TPU v7x, 32 devices: a whole 2x2x4 slice. The times are simulated.
32 devices in a mesh: gx: 2 (over x), gy: 4 (over z), gz: 4 (over y, core).
Axes of the slice: x: 2, y: 2, z: 4, core: 2. Of those that a mesh axis runs over, the one named last changes fastest.
Arguments:
- right_side: float32 [16, 64, 512], P('gx', 'gy', 'gz'), may hold values from -40 to 40
- fiber_class: int32 [16, 64, 512], P('gx', 'gy', 'gz'), may hold values from 0 to 15
- conductivity_scale: float32 [16, 64, 512], P('gx', 'gy', 'gz'), may hold values from 0.8 to 1.25
- class_tensor: float32 [6, 16], replicated, may hold values from -0.15 to 1.8, as said below
- block_ids: int32 [2, 4, 8], replicated, may hold values from 0 to 63, as said below
Outputs:
- solution: float32 [16, 64, 512], P('gx', 'gy', 'gz')
- residual: float32 [16, 64, 512], P('gx', 'gy', 'gz')
Inputs may be any that keep to these rules, and one draw needn't show every extreme that they name: `class_tensor`: column k is the tensor t I + (l - t) f f^T for a unit vector f, with 1 <= t <= 1.5 and 1.05 <= l / t <= 1.2. `block_ids`: each subdomain number names exactly 1 block.
All inputs are finite; a program needn't handle non-finite values.
Results may differ from a plain program's by a relative error of at most 0.0003.
Values sent between devices are 32-bit elements; how exact they have to be, the bound alone decides.
A program may use at most 64 MiB of HBM per device.

v0:
```python
import jax
import jax.numpy as jnp
from jax import lax
from jax.sharding import PartitionSpec as P

CX = 8
CY = 16
CZ = 128
ZBLK = 2
BZ = 64
COARSE = 64
NCLS = 16
ITERS = 2
STENCIL_TAPS = (
    (1, 0, 0, 0, 1.0),
    (-1, 0, 0, 0, 1.0),
    (0, 1, 0, 1, 1.0),
    (0, -1, 0, 1, 1.0),
    (0, 0, 1, 2, 1.0),
    (0, 0, -1, 2, 1.0),
    (1, 1, 0, 3, 0.5),
    (-1, -1, 0, 3, 0.5),
    (1, -1, 0, 3, -0.5),
    (-1, 1, 0, 3, -0.5),
    (1, 0, 1, 4, 0.5),
    (-1, 0, -1, 4, 0.5),
    (1, 0, -1, 4, -0.5),
    (-1, 0, 1, 4, -0.5),
    (0, 1, 1, 5, 0.5),
    (0, -1, -1, 5, 0.5),
    (0, 1, -1, 5, -0.5),
    (0, -1, 1, 5, -0.5),
)


def padded_2(cells, sides, width):
    for axis, dim in sides:
        count = lax.axis_size(axis)
        ends = count - 1
        head = lax.slice_in_dim(cells, 0, width, axis=dim)
        tail = lax.slice_in_dim(cells, cells.shape[dim] - width, cells.shape[dim], axis=dim)
        cells = jnp.concatenate(
            [
                lax.ppermute(tail, axis, [(i, (i + 1) % count) for i in range(ends)]),
                cells,
                lax.ppermute(head, axis, [((i + 1) % count, i) for i in range(ends)]),
            ],
            axis=dim,
        )
    return cells


def shifted(padded, step_x, step_y, step_z):
    width_x = padded.shape[-3] - 2
    width_y = padded.shape[-2] - 2
    width_z = padded.shape[-1] - 2
    return padded[
        1 + step_x : 1 + step_x + width_x,
        1 + step_y : 1 + step_y + width_y,
        1 + step_z : 1 + step_z + width_z,
    ]


def edge_weights(tensors, step_x, step_y, step_z, component, factor):
    layer = tensors[component]
    return 0.5 * factor * (shifted(layer, 0, 0, 0) + shifted(layer, step_x, step_y, step_z))


def operate(padded, tensors):
    centre = shifted(padded, 0, 0, 0)
    accumulated = jnp.zeros_like(centre)
    for step_x, step_y, step_z, component, factor in STENCIL_TAPS:
        weight = edge_weights(tensors, step_x, step_y, step_z, component, factor)
        accumulated = accumulated + weight * (centre - shifted(padded, step_x, step_y, step_z))
    return accumulated


def class_onehot(labels, count):
    return (labels[..., None] == jnp.arange(count, dtype=jnp.int32)).astype(jnp.float32)


def reach_onehot(length, offset):
    position = jnp.arange(length, dtype=jnp.int32)
    relative = (position + offset) // length + 1
    return (relative[:, None] == jnp.arange(3, dtype=jnp.int32)[None, :]).astype(jnp.float32)


def reach_blocks(length, offset, blocks):
    block_span = length // blocks
    position = jnp.arange(length, dtype=jnp.int32)
    owning = (position // block_span)[:, None] == jnp.arange(blocks, dtype=jnp.int32)[None, :]
    relative = ((position % block_span + offset) // block_span + 1)[:, None] == jnp.arange(
        3, dtype=jnp.int32
    )[None, :]
    return (owning[:, :, None] & relative[:, None, :]).astype(jnp.float32)


def centre_mask():
    places = jnp.arange(3, dtype=jnp.int32)
    return (
        (places[:, None, None] == 1) & (places[None, :, None] == 1) & (places[None, None, :] == 1)
    )


def build_tensors(matches, scale, class_tensor):
    return (
        jnp.stack(
            [
                jnp.sum(
                    jnp.where(matches, class_tensor[component][:, None, None, None], 0.0), axis=0
                )
                for component in range(6)
            ]
        )
        * scale[None]
    )


def body(right_side, fiber_class, conductivity_scale, class_tensor, block_ids):
    highest = lax.Precision.HIGHEST
    kinds = jnp.arange(NCLS, dtype=jnp.int32)
    matches = fiber_class[None] == kinds[:, None, None, None]
    local_tensor = build_tensors(matches, conductivity_scale, class_tensor)
    tensors = padded_2(local_tensor, (("gx", 1), ("gy", 2), ("gz", 3)), 1)
    place_x = lax.axis_index("gx")
    place_y = lax.axis_index("gy")
    place_z = lax.axis_index("gz")
    padded_ids = jnp.pad(block_ids, 1, constant_values=-1)
    window = lax.dynamic_slice(padded_ids, (place_x, place_y, place_z * ZBLK), (3, 3, ZBLK + 2))
    own_hot = class_onehot(window[1, 1, 1 : ZBLK + 1], COARSE)
    neighbours = jnp.stack([window[:, :, z_block : z_block + 3] for z_block in range(ZBLK)])
    rim_weight = jnp.zeros((ZBLK, 3, 3, 3), jnp.float32)
    for step_x, step_y, step_z, component, factor in STENCIL_TAPS:
        weight = edge_weights(tensors, step_x, step_y, step_z, component, factor)
        rim_weight = rim_weight + jnp.einsum(
            "xyz,xa,yb,zjc->jabc",
            weight,
            reach_onehot(CX, step_x),
            reach_onehot(CY, step_y),
            reach_blocks(CZ, step_z, ZBLK),
            precision=highest,
        )
    rim_weight = jnp.where(centre_mask()[None], 0.0, rim_weight)
    diagonal_terms = jnp.einsum(
        "jk,j->k", own_hot, jnp.sum(rim_weight, axis=(1, 2, 3)), precision=highest
    )
    coupling = jnp.einsum(
        "jk,jabc,jabcl->kl",
        own_hot,
        rim_weight,
        class_onehot(neighbours, COARSE),
        precision=highest,
    )
    coarse = lax.psum(jnp.diag(diagonal_terms) - coupling, ("gx", "gy", "gz"))
    coarse = 0.5 * (coarse + coarse.T)
    factor_lower = jnp.linalg.cholesky(coarse)

    def restrict(field):
        block_totals = jnp.sum(field.reshape(CX, CY, ZBLK, BZ), axis=(0, 1, 3))
        return jnp.einsum("jk,j->k", own_hot, block_totals, precision=highest)

    def prolong(coarse_values):
        values = jnp.einsum("jk,k->j", own_hot, coarse_values, precision=highest)
        return jnp.broadcast_to(values[None, None, :, None], (CX, CY, ZBLK, BZ)).reshape(CX, CY, CZ)

    def apply_field(field):
        padded = padded_2(field, (("gx", 0), ("gy", 1), ("gz", 2)), 1)
        return operate(padded, tensors)

    def coarse_solve(field):
        projected = lax.psum(restrict(field), ("gx", "gy", "gz"))
        return jax.scipy.linalg.cho_solve((factor_lower, True), projected)

    def deflation_image(coarse_values):
        result = apply_field(prolong(coarse_values))
        return result

    coarse_values = coarse_solve(right_side)
    coarse_part = prolong(coarse_values)
    residual = right_side - deflation_image(coarse_values)
    estimate = jnp.zeros_like(right_side)

    def joint_terms(field):
        product = apply_field(field)
        projected, norm_value, cross_value = lax.psum(
            (restrict(product), jnp.sum(field * field), jnp.sum(field * product)),
            ("gx", "gy", "gz"),
        )
        correction = jax.scipy.linalg.cho_solve((factor_lower, True), projected)
        image_field = product - deflation_image(correction)
        return (image_field, norm_value, cross_value - jnp.sum(projected * correction))

    image_field, norm_now, curvature_now = joint_terms(residual)
    step_size = norm_now / curvature_now
    direction = residual
    along = image_field
    for iteration in range(ITERS):
        estimate = estimate + step_size * direction
        residual = residual - step_size * along
        if iteration + 1 < ITERS:
            image_field, norm_next, curvature_now = joint_terms(residual)
            step_ratio = norm_next / norm_now
            step_size = norm_next / (curvature_now - step_ratio * norm_next / step_size)
            direction = residual + step_ratio * direction
            along = image_field + step_ratio * along
            norm_now = norm_next
    solution = coarse_part + estimate - prolong(coarse_solve(apply_field(estimate)))
    return (solution, residual)


def solution(mesh):
    placed = (P("gx", "gy", "gz"), P("gx", "gy", "gz"), P("gx", "gy", "gz"), P(), P())
    return jax.shard_map(
        body,
        mesh=mesh,
        in_specs=placed,
        out_specs=(P("gx", "gy", "gz"), P("gx", "gy", "gz")),
        check_vma=False,
    )
```

profile of v0, /device:TPU:0, one launch (start us, length us, event | category | flops | bytes accessed | tf_op | source)
XLA Modules:
  0.0 365.0 jit_solution(11324183408643841926)
XLA Ops:
  0.6 0.9 slice_bitcast_fusion.11
  1.6 1.7 select_reduce_fusion
  4.2 4.9 %collective-permute-start = (f32[6,1,16,128]{3,2,1,0:T(8,128)S(1)}, f32[6,1,16,128]{3,2,1,0:T(8,128)S(1)}, u32[]{:S(2)}, u32[]{:S(2)}) collective-permute-start(f32[6,1,16,128]{3,2,1,0:T(8,128)S(1)} %get-tuple-element.39), channel_id=1, source_target_pairs={{0,16},{1,17},{2,18},{3,19},{4,20},{5,21},{6,22},{7,23},{8,24},{9,... | collective-permute-start | bytes 147464 | tf_op jit(solution)/shard_map/ppermute | solution.py:44
  9.1 1.3 collective-permute-start.1
  11.4 3.7 %collective-permute-done.1 = f32[6,1,16,128]{3,2,1,0:T(8,128)S(1)} collective-permute-done((f32[6,1,16,128]{3,2,1,0:T(8,128)S(1)}, f32[6,1,16,128]{3,2,1,0:T(8,128)S(1)}, u32[]{:S(2)}, u32[]{:S(2)}) %collective-permute-start.1) | collective-permute-done | bytes 49184 | tf_op jit(solution)/shard_map/ppermute | solution.py:46
  15.1 3.5 collective-permute-start.2
  18.6 1.3 collective-permute-start.3
  20.2 4.2 %collective-permute-done.3 = f32[6,10,1,128]{3,2,1,0:T(1,128)S(1)} collective-permute-done((f32[6,10,1,128]{3,2,1,0:T(1,128)S(1)}, f32[6,10,1,128]{3,2,1,0:T(1,128)S(1)}, u32[]{:S(2)}, u32[]{:S(2)}) %collective-permute-start.3) | collective-permute-done | bytes 30752 | tf_op jit(solution)/shard_map/ppermute | solution.py:46
  25.2 1.3 collective-permute-start.4
  27.0 1.3 collective-permute-start.5
  28.8 3.0 collective-permute-done.5
  43.4 40.4 %all-reduce.3 = (f32[64,64]{1,0:T(8,128)S(1)}, f32[64]{0:T(128)S(1)}) all-reduce(f32[64,64]{1,0:T(8,128)S(1)} %convolution_subtract_fusion, f32[64]{0:T(128)S(1)} %convolution_bitcast_fusion.26), channel_id=1, replica_groups=mesh['gx'=2,'gy'=4,'gz'=4] {'gx','gy','gz'}, use_global_device_ids=true, to_apply=%region_7.8 | all-reduce | flops 4160 | bytes 33280 | tf_op jit(solution)/shard_map/psum | solution.py:154
  84.0 5.8 %cholesky.19 = f32[64,64]{1,0:T(8,128)S(1)} custom-call(f32[64,64]{1,0:T(8,128)S(1)} %fusion.262), custom_call_target="Cholesky" | custom-call | tf_op jit(solution)/shard_map/jit(cholesky)/cholesky | solution.py:156
  91.2 4.9 %custom-call.11 = f32[1,64,64]{1,2,0:T(8,128)S(1)} custom-call(f32[1,64,64]{2,1,0:T(8,128)S(1)} %fusion.251), custom_call_target="InvertDiagBlocksLowerTriangular" | custom-call | tf_op jit(solution)/shard_map/jit(_cho_solve)/triangular_solve | solution.py:172
  96.8 1.3 collective-permute-start.6
  98.1 4.5 %collective-permute-start.7 = (f32[1,16,128]{2,1,0:T(8,128)S(1)}, f32[1,16,128]{2,1,0:T(8,128)S(1)}, u32[]{:S(2)}, u32[]{:S(2)}) collective-permute-start(f32[1,16,128]{2,1,0:T(8,128)S(1)} %slice.1082), channel_id=1, source_target_pairs={{0,16},{1,17},{2,18},{3,19},{4,20},{5,21},{6,22},{7,23},{8,24},{9,... | collective-permute-start | bytes 24584 | tf_op jit(solution)/shard_map/ppermute | solution.py:44
  102.6 1.3 collective-permute-done.7
  104.0 1.3 collective-permute-start.8
  105.3 4.5 %collective-permute-start.9 = (f32[10,1,128]{2,1,0:T(1,128)S(1)}, f32[10,1,128]{2,1,0:T(1,128)S(1)}, u32[]{:S(2)}, u32[]{:S(2)}) collective-permute-start(f32[10,1,128]{2,1,0:T(1,128)S(1)} %get-tuple-element.105), channel_id=1, source_target_pairs={{0,4},{4,8},{8,12},{1,5},{5,9},{9,13},{2,6},{6,10},{10,14},{3,7},{... | collective-permute-start | bytes 15368 | tf_op jit(solution)/shard_map/ppermute | solution.py:44
  109.9 1.3 collective-permute-done.9
  111.3 1.3 collective-permute-start.10
  112.6 3.0 collective-permute-start.11
  115.7 0.9 collective-permute-done.11
  117.0 1.3 collective-permute-start.12
  118.3 4.5 %collective-permute-start.13 = (f32[1,16,128]{2,1,0:T(8,128)S(1)}, f32[1,16,128]{2,1,0:T(8,128)S(1)}, u32[]{:S(2)}, u32[]{:S(2)}) collective-permute-start(f32[1,16,128]{2,1,0:T(8,128)S(1)} %get-tuple-element.111), channel_id=1, source_target_pairs={{0,16},{1,17},{2,18},{3,19},{4,20},{5,21},{6,22},{7,23},{8,24},{9,... | collective-permute-start | bytes 24584 | tf_op jit(solution)/shard_map/ppermute | solution.py:44
  122.9 1.3 collective-permute-done.13
  124.2 1.3 collective-permute-start.14
  125.5 4.8 %collective-permute-start.15 = (f32[10,1,128]{2,1,0:T(1,128)S(1)}, f32[10,1,128]{2,1,0:T(1,128)S(1)}, u32[]{:S(2)}, u32[]{:S(2)}) collective-permute-start(f32[10,1,128]{2,1,0:T(1,128)S(1)} %get-tuple-element.101), channel_id=1, source_target_pairs={{0,4},{4,8},{8,12},{1,5},{5,9},{9,13},{2,6},{6,10},{10,14},{3,7},{... | collective-permute-start | bytes 15368 | tf_op jit(solution)/shard_map/ppermute | solution.py:44
  130.3 1.3 collective-permute-done.15
  131.8 1.3 collective-permute-start.16
  133.1 3.3 collective-permute-start.17
  136.5 0.9 collective-permute-done.17
  138.8 48.9 %all-reduce.2 = (f32[64]{0:T(128)S(1)}, f32[]{:T(128)}, f32[]{:T(128)}) all-reduce(f32[64]{0:T(128)S(1)} %convolution_bitcast_fusion.24, f32[]{:T(128)} %get-tuple-element.10, f32[]{:T(128)} %get-tuple-element.8), channel_id=1, replica_groups=mesh['gx'=2,'gy'=4,'gz'=4] {'gx','gy','gz'}, use_global_device_ids=true, to_apply=%region_19.21 | all-reduce | flops 66 | bytes 528 | tf_op jit(solution)/shard_map/psum | solution.py:185
  189.0 1.3 collective-permute-start.18
  190.3 4.5 %collective-permute-start.19 = (f32[1,16,128]{2,1,0:T(8,128)S(1)}, f32[1,16,128]{2,1,0:T(8,128)S(1)}, u32[]{:S(2)}, u32[]{:S(2)}) collective-permute-start(f32[1,16,128]{2,1,0:T(8,128)S(1)} %slice.1129), channel_id=1, source_target_pairs={{0,16},{1,17},{2,18},{3,19},{4,20},{5,21},{6,22},{7,23},{8,24},{9,... | collective-permute-start | bytes 24584 | tf_op jit(solution)/shard_map/ppermute | solution.py:44
  194.9 1.3 collective-permute-done.19
  196.2 1.3 collective-permute-start.20
  197.5 4.5 %collective-permute-start.21 = (f32[10,1,128]{2,1,0:T(1,128)S(1)}, f32[10,1,128]{2,1,0:T(1,128)S(1)}, u32[]{:S(2)}, u32[]{:S(2)}) collective-permute-start(f32[10,1,128]{2,1,0:T(1,128)S(1)} %get-tuple-element.97), channel_id=1, source_target_pairs={{0,4},{4,8},{8,12},{1,5},{5,9},{9,13},{2,6},{6,10},{10,14},{3,7},{... | collective-permute-start | bytes 15368 | tf_op jit(solution)/shard_map/ppermute | solution.py:44
  204.2 1.3 collective-permute-start.22
  205.5 3.0 collective-permute-start.23
  208.6 0.9 collective-permute-done.23
  209.9 1.3 collective-permute-start.24
  211.2 4.5 %collective-permute-start.25 = (f32[1,16,128]{2,1,0:T(8,128)S(1)}, f32[1,16,128]{2,1,0:T(8,128)S(1)}, u32[]{:S(2)}, u32[]{:S(2)}) collective-permute-start(f32[1,16,128]{2,1,0:T(8,128)S(1)} %get-tuple-element.109), channel_id=1, source_target_pairs={{0,16},{1,17},{2,18},{3,19},{4,20},{5,21},{6,22},{7,23},{8,24},{9,... | collective-permute-start | bytes 24584 | tf_op jit(solution)/shard_map/ppermute | solution.py:44
  215.7 1.3 collective-permute-done.25
  217.1 1.3 collective-permute-start.26
  218.4 4.5 %collective-permute-start.27 = (f32[10,1,128]{2,1,0:T(1,128)S(1)}, f32[10,1,128]{2,1,0:T(1,128)S(1)}, u32[]{:S(2)}, u32[]{:S(2)}) collective-permute-start(f32[10,1,128]{2,1,0:T(1,128)S(1)} %get-tuple-element.93), channel_id=1, source_target_pairs={{0,4},{4,8},{8,12},{1,5},{5,9},{9,13},{2,6},{6,10},{10,14},{3,7},{... | collective-permute-start | bytes 15368 | tf_op jit(solution)/shard_map/ppermute | solution.py:44
  223.0 1.3 collective-permute-done.27
  224.4 1.3 collective-permute-start.28
  225.7 3.2 collective-permute-start.29
  229.0 0.9 collective-permute-done.29
  231.3 48.6 %all-reduce.1 = (f32[]{:T(128)}, f32[]{:T(128)}, f32[64]{0:T(128)S(1)}) all-reduce(f32[]{:T(128)} %get-tuple-element.7, f32[]{:T(128)} %get-tuple-element.6, f32[64]{0:T(128)S(1)} %convolution_bitcast_fusion.22), channel_id=1, replica_groups=mesh['gx'=2,'gy'=4,'gz'=4] {'gx','gy','gz'}, use_global_device_ids=true, to_apply=%region_22.24 | all-reduce | flops 66 | bytes 528 | tf_op jit(solution)/shard_map/psum | solution.py:185
  281.3 1.3 collective-permute-start.36
  282.6 4.5 %collective-permute-start.37 = (f32[1,16,128]{2,1,0:T(8,128)S(1)}, f32[1,16,128]{2,1,0:T(8,128)S(1)}, u32[]{:S(2)}, u32[]{:S(2)}) collective-permute-start(f32[1,16,128]{2,1,0:T(8,128)S(1)} %slice.1200), channel_id=1, source_target_pairs={{0,16},{1,17},{2,18},{3,19},{4,20},{5,21},{6,22},{7,23},{8,24},{9,... | collective-permute-start | bytes 24584 | tf_op jit(solution)/shard_map/ppermute | solution.py:44
  291.7 1.3 collective-permute-start.30
  293.0 4.5 %collective-permute-start.31 = (f32[1,16,128]{2,1,0:T(8,128)S(1)}, f32[1,16,128]{2,1,0:T(8,128)S(1)}, u32[]{:S(2)}, u32[]{:S(2)}) collective-permute-start(f32[1,16,128]{2,1,0:T(8,128)S(1)} %get-tuple-element.107), channel_id=1, source_target_pairs={{0,16},{1,17},{2,18},{3,19},{4,20},{5,21},{6,22},{7,23},{8,24},{9,... | collective-permute-start | bytes 24584 | tf_op jit(solution)/shard_map/ppermute | solution.py:44
  297.6 1.3 collective-permute-start.38
  298.9 4.5 %collective-permute-start.39 = (f32[10,1,128]{2,1,0:T(1,128)S(1)}, f32[10,1,128]{2,1,0:T(1,128)S(1)}, u32[]{:S(2)}, u32[]{:S(2)}) collective-permute-start(f32[10,1,128]{2,1,0:T(1,128)S(1)} %get-tuple-element.85), channel_id=1, source_target_pairs={{0,4},{4,8},{8,12},{1,5},{5,9},{9,13},{2,6},{6,10},{10,14},{3,7},{... | collective-permute-start | bytes 15368 | tf_op jit(solution)/shard_map/ppermute | solution.py:44
  303.5 1.3 collective-permute-start.32
  304.8 4.5 %collective-permute-start.33 = (f32[10,1,128]{2,1,0:T(1,128)S(1)}, f32[10,1,128]{2,1,0:T(1,128)S(1)}, u32[]{:S(2)}, u32[]{:S(2)}) collective-permute-start(f32[10,1,128]{2,1,0:T(1,128)S(1)} %get-tuple-element.89), channel_id=1, source_target_pairs={{0,4},{4,8},{8,12},{1,5},{5,9},{9,13},{2,6},{6,10},{10,14},{3,7},{... | collective-permute-start | bytes 15368 | tf_op jit(solution)/shard_map/ppermute | solution.py:44
  309.5 1.3 collective-permute-start.40
  310.8 3.0 collective-permute-start.41
  314.0 1.3 collective-permute-start.34
  315.3 4.7 %collective-permute-start.35 = (f32[10,18,1]{2,1,0:T(8,128)S(1)}, f32[10,18,1]{2,1,0:T(8,128)S(1)}, u32[]{:S(2)}, u32[]{:S(2)}) collective-permute-start(f32[10,18,1]{2,1,0:T(8,128)S(1)} %get-tuple-element.61), channel_id=1, source_target_pairs={{0,1},{1,2},{2,3},{4,5},{5,6},{6,7},{8,9},{9,10},{10,11},{12,13},{... | collective-permute-start | bytes 2168 | tf_op jit(solution)/shard_map/ppermute | solution.py:44
  321.7 40.9 %psum.71 = f32[64]{0:T(128)S(1)} all-reduce(f32[64]{0:T(128)S(1)} %convolution_bitcast_fusion.21), channel_id=1, replica_groups=mesh['gx'=2,'gy'=4,'gz'=4] {'gx','gy','gz'}, use_global_device_ids=true, to_apply=%region_31.33 | all-reduce | flops 64 | bytes 512 | tf_op jit(solution)/shard_map/psum | solution.py:171
  (216 shorter events, 28.7 us)
Async XLA Ops:
  0.6 10.1 %copy-start = (f32[8,16,128]{2,1,0:T(8,128)S(1)}, f32[8,16,128]{2,1,0:T(8,128)}, u32[]{:S(2)}) copy-start(f32[8,16,128]{2,1,0:T(8,128)} %param.7) | copy-start | bytes 196612
  0.6 10.3 %copy-start.1 = (s32[2,4,8]{2,1,0:T(4,128)S(1)}, s32[2,4,8]{2,1,0:T(4,128)}, u32[]{:S(2)}) copy-start(s32[2,4,8]{2,1,0:T(4,128)} %param.11) | copy-start | bytes 772
  4.2 7.1 %collective-permute-start = (f32[6,1,16,128]{3,2,1,0:T(8,128)S(1)}, f32[6,1,16,128]{3,2,1,0:T(8,128)S(1)}, u32[]{:S(2)}, u32[]{:S(2)}) collective-permute-start(f32[6,1,16,128]{3,2,1,0:T(8,128)S(1)} %get-tuple-element.39), channel_id=1, source_target_pairs={{0,16},{1,17},{2,18},{3,19},{4,20},{5,21},{6,22},{7,23},{8,24},{9,... | collective-permute-start | bytes 147464 | tf_op jit(solution)/shard_map/ppermute | solution.py:44
  9.1 6.0 %collective-permute-start.1 = (f32[6,1,16,128]{3,2,1,0:T(8,128)S(1)}, f32[6,1,16,128]{3,2,1,0:T(8,128)S(1)}, u32[]{:S(2)}, u32[]{:S(2)}) collective-permute-start(f32[6,1,16,128]{3,2,1,0:T(8,128)S(1)} %get-tuple-element.40), channel_id=1, source_target_pairs={{16,0},{17,1},{18,2},{19,3},{20,4},{21,5},{22,6},{23,7},{24,8},{25... | collective-permute-start | bytes 147464 | tf_op jit(solution)/shard_map/ppermute | solution.py:46
  15.1 5.0 %collective-permute-start.2 = (f32[6,10,1,128]{3,2,1,0:T(1,128)S(1)}, f32[6,10,1,128]{3,2,1,0:T(1,128)S(1)}, u32[]{:S(2)}, u32[]{:S(2)}) collective-permute-start(f32[6,10,1,128]{3,2,1,0:T(1,128)S(1)} %get-tuple-element.37), channel_id=1, source_target_pairs={{0,4},{4,8},{8,12},{1,5},{5,9},{9,13},{2,6},{6,10},{10,14},{3,7},{... | collective-permute-start | bytes 92168 | tf_op jit(solution)/shard_map/ppermute | solution.py:44
  18.6 5.8 %collective-permute-start.3 = (f32[6,10,1,128]{3,2,1,0:T(1,128)S(1)}, f32[6,10,1,128]{3,2,1,0:T(1,128)S(1)}, u32[]{:S(2)}, u32[]{:S(2)}) collective-permute-start(f32[6,10,1,128]{3,2,1,0:T(1,128)S(1)} %get-tuple-element.38), channel_id=1, source_target_pairs={{4,0},{8,4},{12,8},{5,1},{9,5},{13,9},{6,2},{10,6},{14,10},{7,3},{... | collective-permute-start | bytes 92168 | tf_op jit(solution)/shard_map/ppermute | solution.py:46
  25.2 3.1 collective-permute-start.4
  27.0 4.8 %collective-permute-start.5 = (f32[6,10,18,1]{2,3,1,0:T(1,128)S(1)}, f32[6,10,18,1]{2,3,1,0:T(1,128)S(1)}, u32[]{:S(2)}, u32[]{:S(2)}) collective-permute-start(f32[6,10,18,1]{2,3,1,0:T(1,128)S(1)} %copy.84), channel_id=1, source_target_pairs={{1,0},{2,1},{3,2},{5,4},{6,5},{7,6},{9,8},{10,9},{11,10},{13,12},{... | collective-permute-start | bytes 12968 | tf_op jit(solution)/shard_map/ppermute | solution.py:46
  96.8 5.9 %collective-permute-start.6 = (f32[1,16,128]{2,1,0:T(8,128)S(1)}, f32[1,16,128]{2,1,0:T(8,128)S(1)}, u32[]{:S(2)}, u32[]{:S(2)}) collective-permute-start(f32[1,16,128]{2,1,0:T(8,128)S(1)} %slice.1082), channel_id=1, source_target_pairs={{16,0},{17,1},{18,2},{19,3},{20,4},{21,5},{22,6},{23,7},{24,8},{25... | collective-permute-start | bytes 24584 | tf_op jit(solution)/shard_map/ppermute | solution.py:46
  98.1 5.9 %collective-permute-start.7 = (f32[1,16,128]{2,1,0:T(8,128)S(1)}, f32[1,16,128]{2,1,0:T(8,128)S(1)}, u32[]{:S(2)}, u32[]{:S(2)}) collective-permute-start(f32[1,16,128]{2,1,0:T(8,128)S(1)} %slice.1082), channel_id=1, source_target_pairs={{0,16},{1,17},{2,18},{3,19},{4,20},{5,21},{6,22},{7,23},{8,24},{9,... | collective-permute-start | bytes 24584 | tf_op jit(solution)/shard_map/ppermute | solution.py:44
  104.0 5.9 %collective-permute-start.8 = (f32[10,1,128]{2,1,0:T(1,128)S(1)}, f32[10,1,128]{2,1,0:T(1,128)S(1)}, u32[]{:S(2)}, u32[]{:S(2)}) collective-permute-start(f32[10,1,128]{2,1,0:T(1,128)S(1)} %get-tuple-element.106), channel_id=1, source_target_pairs={{4,0},{8,4},{12,8},{5,1},{9,5},{13,9},{6,2},{10,6},{14,10},{7,3},{... | collective-permute-start | bytes 15368 | tf_op jit(solution)/shard_map/ppermute | solution.py:46
  105.3 5.9 %collective-permute-start.9 = (f32[10,1,128]{2,1,0:T(1,128)S(1)}, f32[10,1,128]{2,1,0:T(1,128)S(1)}, u32[]{:S(2)}, u32[]{:S(2)}) collective-permute-start(f32[10,1,128]{2,1,0:T(1,128)S(1)} %get-tuple-element.105), channel_id=1, source_target_pairs={{0,4},{4,8},{8,12},{1,5},{5,9},{9,13},{2,6},{6,10},{10,14},{3,7},{... | collective-permute-start | bytes 15368 | tf_op jit(solution)/shard_map/ppermute | solution.py:44
  111.3 4.4 %collective-permute-start.10 = (f32[10,18,1]{2,1,0:T(8,128)S(1)}, f32[10,18,1]{2,1,0:T(8,128)S(1)}, u32[]{:S(2)}, u32[]{:S(2)}) collective-permute-start(f32[10,18,1]{2,1,0:T(8,128)S(1)} %get-tuple-element.70), channel_id=1, source_target_pairs={{1,0},{2,1},{3,2},{5,4},{6,5},{7,6},{9,8},{10,9},{11,10},{13,12},{... | collective-permute-start | bytes 2168 | tf_op jit(solution)/shard_map/ppermute | solution.py:46
  112.6 4.0 %collective-permute-start.11 = (f32[10,18,1]{2,1,0:T(8,128)S(1)}, f32[10,18,1]{2,1,0:T(8,128)S(1)}, u32[]{:S(2)}, u32[]{:S(2)}) collective-permute-start(f32[10,18,1]{2,1,0:T(8,128)S(1)} %get-tuple-element.69), channel_id=1, source_target_pairs={{0,1},{1,2},{2,3},{4,5},{5,6},{6,7},{8,9},{9,10},{10,11},{12,13},{... | collective-permute-start | bytes 2168 | tf_op jit(solution)/shard_map/ppermute | solution.py:44
  117.0 5.9 %collective-permute-start.12 = (f32[1,16,128]{2,1,0:T(8,128)S(1)}, f32[1,16,128]{2,1,0:T(8,128)S(1)}, u32[]{:S(2)}, u32[]{:S(2)}) collective-permute-start(f32[1,16,128]{2,1,0:T(8,128)S(1)} %get-tuple-element.112), channel_id=1, source_target_pairs={{16,0},{17,1},{18,2},{19,3},{20,4},{21,5},{22,6},{23,7},{24,8},{25... | collective-permute-start | bytes 24584 | tf_op jit(solution)/shard_map/ppermute | solution.py:46
  118.3 5.9 %collective-permute-start.13 = (f32[1,16,128]{2,1,0:T(8,128)S(1)}, f32[1,16,128]{2,1,0:T(8,128)S(1)}, u32[]{:S(2)}, u32[]{:S(2)}) collective-permute-start(f32[1,16,128]{2,1,0:T(8,128)S(1)} %get-tuple-element.111), channel_id=1, source_target_pairs={{0,16},{1,17},{2,18},{3,19},{4,20},{5,21},{6,22},{7,23},{8,24},{9,... | collective-permute-start | bytes 24584 | tf_op jit(solution)/shard_map/ppermute | solution.py:44
  124.2 6.1 %collective-permute-start.14 = (f32[10,1,128]{2,1,0:T(1,128)S(1)}, f32[10,1,128]{2,1,0:T(1,128)S(1)}, u32[]{:S(2)}, u32[]{:S(2)}) collective-permute-start(f32[10,1,128]{2,1,0:T(1,128)S(1)} %get-tuple-element.102), channel_id=1, source_target_pairs={{4,0},{8,4},{12,8},{5,1},{9,5},{13,9},{6,2},{10,6},{14,10},{7,3},{... | collective-permute-start | bytes 15368 | tf_op jit(solution)/shard_map/ppermute | solution.py:46
  125.5 6.1 %collective-permute-start.15 = (f32[10,1,128]{2,1,0:T(1,128)S(1)}, f32[10,1,128]{2,1,0:T(1,128)S(1)}, u32[]{:S(2)}, u32[]{:S(2)}) collective-permute-start(f32[10,1,128]{2,1,0:T(1,128)S(1)} %get-tuple-element.101), channel_id=1, source_target_pairs={{0,4},{4,8},{8,12},{1,5},{5,9},{9,13},{2,6},{6,10},{10,14},{3,7},{... | collective-permute-start | bytes 15368 | tf_op jit(solution)/shard_map/ppermute | solution.py:44
  131.8 4.7 %collective-permute-start.16 = (f32[10,18,1]{2,1,0:T(8,128)S(1)}, f32[10,18,1]{2,1,0:T(8,128)S(1)}, u32[]{:S(2)}, u32[]{:S(2)}) collective-permute-start(f32[10,18,1]{2,1,0:T(8,128)S(1)} %get-tuple-element.68), channel_id=1, source_target_pairs={{1,0},{2,1},{3,2},{5,4},{6,5},{7,6},{9,8},{10,9},{11,10},{13,12},{... | collective-permute-start | bytes 2168 | tf_op jit(solution)/shard_map/ppermute | solution.py:46
  133.1 4.3 %collective-permute-start.17 = (f32[10,18,1]{2,1,0:T(8,128)S(1)}, f32[10,18,1]{2,1,0:T(8,128)S(1)}, u32[]{:S(2)}, u32[]{:S(2)}) collective-permute-start(f32[10,18,1]{2,1,0:T(8,128)S(1)} %get-tuple-element.67), channel_id=1, source_target_pairs={{0,1},{1,2},{2,3},{4,5},{5,6},{6,7},{8,9},{9,10},{10,11},{12,13},{... | collective-permute-start | bytes 2168 | tf_op jit(solution)/shard_map/ppermute | solution.py:44
  189.0 5.8 %collective-permute-start.18 = (f32[1,16,128]{2,1,0:T(8,128)S(1)}, f32[1,16,128]{2,1,0:T(8,128)S(1)}, u32[]{:S(2)}, u32[]{:S(2)}) collective-permute-start(f32[1,16,128]{2,1,0:T(8,128)S(1)} %slice.1129), channel_id=1, source_target_pairs={{16,0},{17,1},{18,2},{19,3},{20,4},{21,5},{22,6},{23,7},{24,8},{25... | collective-permute-start | bytes 24584 | tf_op jit(solution)/shard_map/ppermute | solution.py:46
  190.3 5.9 %collective-permute-start.19 = (f32[1,16,128]{2,1,0:T(8,128)S(1)}, f32[1,16,128]{2,1,0:T(8,128)S(1)}, u32[]{:S(2)}, u32[]{:S(2)}) collective-permute-start(f32[1,16,128]{2,1,0:T(8,128)S(1)} %slice.1129), channel_id=1, source_target_pairs={{0,16},{1,17},{2,18},{3,19},{4,20},{5,21},{6,22},{7,23},{8,24},{9,... | collective-permute-start | bytes 24584 | tf_op jit(solution)/shard_map/ppermute | solution.py:44
  196.2 7.8 %collective-permute-start.20 = (f32[10,1,128]{2,1,0:T(1,128)S(1)}, f32[10,1,128]{2,1,0:T(1,128)S(1)}, u32[]{:S(2)}, u32[]{:S(2)}) collective-permute-start(f32[10,1,128]{2,1,0:T(1,128)S(1)} %get-tuple-element.98), channel_id=1, source_target_pairs={{4,0},{8,4},{12,8},{5,1},{9,5},{13,9},{6,2},{10,6},{14,10},{7,3},{... | collective-permute-start | bytes 15368 | tf_op jit(solution)/shard_map/ppermute | solution.py:46
  197.5 6.5 %collective-permute-start.21 = (f32[10,1,128]{2,1,0:T(1,128)S(1)}, f32[10,1,128]{2,1,0:T(1,128)S(1)}, u32[]{:S(2)}, u32[]{:S(2)}) collective-permute-start(f32[10,1,128]{2,1,0:T(1,128)S(1)} %get-tuple-element.97), channel_id=1, source_target_pairs={{0,4},{4,8},{8,12},{1,5},{5,9},{9,13},{2,6},{6,10},{10,14},{3,7},{... | collective-permute-start | bytes 15368 | tf_op jit(solution)/shard_map/ppermute | solution.py:44
  204.2 4.4 %collective-permute-start.22 = (f32[10,18,1]{2,1,0:T(8,128)S(1)}, f32[10,18,1]{2,1,0:T(8,128)S(1)}, u32[]{:S(2)}, u32[]{:S(2)}) collective-permute-start(f32[10,18,1]{2,1,0:T(8,128)S(1)} %get-tuple-element.66), channel_id=1, source_target_pairs={{1,0},{2,1},{3,2},{5,4},{6,5},{7,6},{9,8},{10,9},{11,10},{13,12},{... | collective-permute-start | bytes 2168 | tf_op jit(solution)/shard_map/ppermute | solution.py:46
  205.5 4.0 %collective-permute-start.23 = (f32[10,18,1]{2,1,0:T(8,128)S(1)}, f32[10,18,1]{2,1,0:T(8,128)S(1)}, u32[]{:S(2)}, u32[]{:S(2)}) collective-permute-start(f32[10,18,1]{2,1,0:T(8,128)S(1)} %get-tuple-element.65), channel_id=1, source_target_pairs={{0,1},{1,2},{2,3},{4,5},{5,6},{6,7},{8,9},{9,10},{10,11},{12,13},{... | collective-permute-start | bytes 2168 | tf_op jit(solution)/shard_map/ppermute | solution.py:44
  209.9 5.9 %collective-permute-start.24 = (f32[1,16,128]{2,1,0:T(8,128)S(1)}, f32[1,16,128]{2,1,0:T(8,128)S(1)}, u32[]{:S(2)}, u32[]{:S(2)}) collective-permute-start(f32[1,16,128]{2,1,0:T(8,128)S(1)} %get-tuple-element.110), channel_id=1, source_target_pairs={{16,0},{17,1},{18,2},{19,3},{20,4},{21,5},{22,6},{23,7},{24,8},{25... | collective-permute-start | bytes 24584 | tf_op jit(solution)/shard_map/ppermute | solution.py:46
  211.2 5.9 %collective-permute-start.25 = (f32[1,16,128]{2,1,0:T(8,128)S(1)}, f32[1,16,128]{2,1,0:T(8,128)S(1)}, u32[]{:S(2)}, u32[]{:S(2)}) collective-permute-start(f32[1,16,128]{2,1,0:T(8,128)S(1)} %get-tuple-element.109), channel_id=1, source_target_pairs={{0,16},{1,17},{2,18},{3,19},{4,20},{5,21},{6,22},{7,23},{8,24},{9,... | collective-permute-start | bytes 24584 | tf_op jit(solution)/shard_map/ppermute | solution.py:44
  217.1 5.9 %collective-permute-start.26 = (f32[10,1,128]{2,1,0:T(1,128)S(1)}, f32[10,1,128]{2,1,0:T(1,128)S(1)}, u32[]{:S(2)}, u32[]{:S(2)}) collective-permute-start(f32[10,1,128]{2,1,0:T(1,128)S(1)} %get-tuple-element.94), channel_id=1, source_target_pairs={{4,0},{8,4},{12,8},{5,1},{9,5},{13,9},{6,2},{10,6},{14,10},{7,3},{... | collective-permute-start | bytes 15368 | tf_op jit(solution)/shard_map/ppermute | solution.py:46
  218.4 5.9 %collective-permute-start.27 = (f32[10,1,128]{2,1,0:T(1,128)S(1)}, f32[10,1,128]{2,1,0:T(1,128)S(1)}, u32[]{:S(2)}, u32[]{:S(2)}) collective-permute-start(f32[10,1,128]{2,1,0:T(1,128)S(1)} %get-tuple-element.93), channel_id=1, source_target_pairs={{0,4},{4,8},{8,12},{1,5},{5,9},{9,13},{2,6},{6,10},{10,14},{3,7},{... | collective-permute-start | bytes 15368 | tf_op jit(solution)/shard_map/ppermute | solution.py:44
  224.4 4.6 %collective-permute-start.28 = (f32[10,18,1]{2,1,0:T(8,128)S(1)}, f32[10,18,1]{2,1,0:T(8,128)S(1)}, u32[]{:S(2)}, u32[]{:S(2)}) collective-permute-start(f32[10,18,1]{2,1,0:T(8,128)S(1)} %get-tuple-element.64), channel_id=1, source_target_pairs={{1,0},{2,1},{3,2},{5,4},{6,5},{7,6},{9,8},{10,9},{11,10},{13,12},{... | collective-permute-start | bytes 2168 | tf_op jit(solution)/shard_map/ppermute | solution.py:46
  225.7 4.2 %collective-permute-start.29 = (f32[10,18,1]{2,1,0:T(8,128)S(1)}, f32[10,18,1]{2,1,0:T(8,128)S(1)}, u32[]{:S(2)}, u32[]{:S(2)}) collective-permute-start(f32[10,18,1]{2,1,0:T(8,128)S(1)} %get-tuple-element.63), channel_id=1, source_target_pairs={{0,1},{1,2},{2,3},{4,5},{5,6},{6,7},{8,9},{9,10},{10,11},{12,13},{... | collective-permute-start | bytes 2168 | tf_op jit(solution)/shard_map/ppermute | solution.py:44
  281.3 16.3 %collective-permute-start.36 = (f32[1,16,128]{2,1,0:T(8,128)S(1)}, f32[1,16,128]{2,1,0:T(8,128)S(1)}, u32[]{:S(2)}, u32[]{:S(2)}) collective-permute-start(f32[1,16,128]{2,1,0:T(8,128)S(1)} %slice.1200), channel_id=1, source_target_pairs={{16,0},{17,1},{18,2},{19,3},{20,4},{21,5},{22,6},{23,7},{24,8},{25... | collective-permute-start | bytes 24584 | tf_op jit(solution)/shard_map/ppermute | solution.py:46
  282.6 15.0 %collective-permute-start.37 = (f32[1,16,128]{2,1,0:T(8,128)S(1)}, f32[1,16,128]{2,1,0:T(8,128)S(1)}, u32[]{:S(2)}, u32[]{:S(2)}) collective-permute-start(f32[1,16,128]{2,1,0:T(8,128)S(1)} %slice.1200), channel_id=1, source_target_pairs={{0,16},{1,17},{2,18},{3,19},{4,20},{5,21},{6,22},{7,23},{8,24},{9,... | collective-permute-start | bytes 24584 | tf_op jit(solution)/shard_map/ppermute | solution.py:44
  291.7 11.8 %collective-permute-start.30 = (f32[1,16,128]{2,1,0:T(8,128)S(1)}, f32[1,16,128]{2,1,0:T(8,128)S(1)}, u32[]{:S(2)}, u32[]{:S(2)}) collective-permute-start(f32[1,16,128]{2,1,0:T(8,128)S(1)} %get-tuple-element.108), channel_id=1, source_target_pairs={{16,0},{17,1},{18,2},{19,3},{20,4},{21,5},{22,6},{23,7},{24,8},{25... | collective-permute-start | bytes 24584 | tf_op jit(solution)/shard_map/ppermute | solution.py:46
  293.0 10.5 %collective-permute-start.31 = (f32[1,16,128]{2,1,0:T(8,128)S(1)}, f32[1,16,128]{2,1,0:T(8,128)S(1)}, u32[]{:S(2)}, u32[]{:S(2)}) collective-permute-start(f32[1,16,128]{2,1,0:T(8,128)S(1)} %get-tuple-element.107), channel_id=1, source_target_pairs={{0,16},{1,17},{2,18},{3,19},{4,20},{5,21},{6,22},{7,23},{8,24},{9,... | collective-permute-start | bytes 24584 | tf_op jit(solution)/shard_map/ppermute | solution.py:44
  297.6 11.8 %collective-permute-start.38 = (f32[10,1,128]{2,1,0:T(1,128)S(1)}, f32[10,1,128]{2,1,0:T(1,128)S(1)}, u32[]{:S(2)}, u32[]{:S(2)}) collective-permute-start(f32[10,1,128]{2,1,0:T(1,128)S(1)} %get-tuple-element.86), channel_id=1, source_target_pairs={{4,0},{8,4},{12,8},{5,1},{9,5},{13,9},{6,2},{10,6},{14,10},{7,3},{... | collective-permute-start | bytes 15368 | tf_op jit(solution)/shard_map/ppermute | solution.py:46
  298.9 10.5 %collective-permute-start.39 = (f32[10,1,128]{2,1,0:T(1,128)S(1)}, f32[10,1,128]{2,1,0:T(1,128)S(1)}, u32[]{:S(2)}, u32[]{:S(2)}) collective-permute-start(f32[10,1,128]{2,1,0:T(1,128)S(1)} %get-tuple-element.85), channel_id=1, source_target_pairs={{0,4},{4,8},{8,12},{1,5},{5,9},{9,13},{2,6},{6,10},{10,14},{3,7},{... | collective-permute-start | bytes 15368 | tf_op jit(solution)/shard_map/ppermute | solution.py:44
  303.5 10.3 %collective-permute-start.32 = (f32[10,1,128]{2,1,0:T(1,128)S(1)}, f32[10,1,128]{2,1,0:T(1,128)S(1)}, u32[]{:S(2)}, u32[]{:S(2)}) collective-permute-start(f32[10,1,128]{2,1,0:T(1,128)S(1)} %get-tuple-element.90), channel_id=1, source_target_pairs={{4,0},{8,4},{12,8},{5,1},{9,5},{13,9},{6,2},{10,6},{14,10},{7,3},{... | collective-permute-start | bytes 15368 | tf_op jit(solution)/shard_map/ppermute | solution.py:46
  304.8 9.1 %collective-permute-start.33 = (f32[10,1,128]{2,1,0:T(1,128)S(1)}, f32[10,1,128]{2,1,0:T(1,128)S(1)}, u32[]{:S(2)}, u32[]{:S(2)}) collective-permute-start(f32[10,1,128]{2,1,0:T(1,128)S(1)} %get-tuple-element.89), channel_id=1, source_target_pairs={{0,4},{4,8},{8,12},{1,5},{5,9},{9,13},{2,6},{6,10},{10,14},{3,7},{... | collective-permute-start | bytes 15368 | tf_op jit(solution)/shard_map/ppermute | solution.py:44
  309.5 54.4 %collective-permute-start.40 = (f32[10,18,1]{2,1,0:T(8,128)S(1)}, f32[10,18,1]{2,1,0:T(8,128)S(1)}, u32[]{:S(2)}, u32[]{:S(2)}) collective-permute-start(f32[10,18,1]{2,1,0:T(8,128)S(1)} %get-tuple-element.60), channel_id=1, source_target_pairs={{1,0},{2,1},{3,2},{5,4},{6,5},{7,6},{9,8},{10,9},{11,10},{13,12},{... | collective-permute-start | bytes 2168 | tf_op jit(solution)/shard_map/ppermute | solution.py:46
  310.8 53.1 %collective-permute-start.41 = (f32[10,18,1]{2,1,0:T(8,128)S(1)}, f32[10,18,1]{2,1,0:T(8,128)S(1)}, u32[]{:S(2)}, u32[]{:S(2)}) collective-permute-start(f32[10,18,1]{2,1,0:T(8,128)S(1)} %get-tuple-element.59), channel_id=1, source_target_pairs={{0,1},{1,2},{2,3},{4,5},{5,6},{6,7},{8,9},{9,10},{10,11},{12,13},{... | collective-permute-start | bytes 2168 | tf_op jit(solution)/shard_map/ppermute | solution.py:44
  314.0 6.0 %collective-permute-start.34 = (f32[10,18,1]{2,1,0:T(8,128)S(1)}, f32[10,18,1]{2,1,0:T(8,128)S(1)}, u32[]{:S(2)}, u32[]{:S(2)}) collective-permute-start(f32[10,18,1]{2,1,0:T(8,128)S(1)} %get-tuple-element.62), channel_id=1, source_target_pairs={{1,0},{2,1},{3,2},{5,4},{6,5},{7,6},{9,8},{10,9},{11,10},{13,12},{... | collective-permute-start | bytes 2168 | tf_op jit(solution)/shard_map/ppermute | solution.py:46
  315.3 5.6 %collective-permute-start.35 = (f32[10,18,1]{2,1,0:T(8,128)S(1)}, f32[10,18,1]{2,1,0:T(8,128)S(1)}, u32[]{:S(2)}, u32[]{:S(2)}) collective-permute-start(f32[10,18,1]{2,1,0:T(8,128)S(1)} %get-tuple-element.61), channel_id=1, source_target_pairs={{0,1},{1,2},{2,3},{4,5},{5,6},{6,7},{8,9},{9,10},{10,11},{12,13},{... | collective-permute-start | bytes 2168 | tf_op jit(solution)/shard_map/ppermute | solution.py:44
where the time goes:
time: 367 us; the launch traced here: 365 us
  blocking collectives  179 us (49%)
  starting transfers between devices  112 us (31%)
  waiting for transfers between devices  25.1 us (7%)
  other arithmetic  22.3 us (6%)
  matrix products  13.4 us (4%)
  between operations  8.31 us (2%)
  local copies, waits for them, and re-layouts  5.09 us (1%)
    psum x2, blocking collectives, joint_terms(): lax.psum((restrict(product), jnp.sum(field * field), jnp.sum(field * prod...  97.5 us
    ppermute x21, starting transfers between devices, padded_2(): lax.ppermute(tail, axis, [(i, (i + 1) % count) for i in range(ends)])  84.8 us
    psum x1, blocking collectives, coarse_solve(): projected = lax.psum(restrict(field), ('gx', 'gy', 'gz'))  40.9 us
    psum x1, blocking collectives, body(): coarse = lax.psum(jnp.diag(diagonal_terms) - coupling, ('gx', 'gy', 'gz'))  40.4 us
    ppermute x21, starting transfers between devices, padded_2(): lax.ppermute(head, axis, [((i + 1) % count, i) for i in range(ends)])  27.1 us
    ppermute x21, waiting for transfers between devices, padded_2(): lax.ppermute(tail, axis, [(i, (i + 1) % count) for i in range(ends)])  14.1 us
    ppermute x21, waiting for transfers between devices, padded_2(): lax.ppermute(head, axis, [((i + 1) % count, i) for i in range(ends)])  11 us
    dot_general x54, matrix products, body(): jnp.einsum('xyz,xa,yb,zjc->jabc', weight, reach_onehot(CX, step_x), reach...  8.59 us
  transfers between devices with their start and end apart: 42, of which 16 were waited for; matrix products, arithmetic and copies ran while one was open for 1% of the time, Pallas kernels for 0%

commit v1 on v0

--- a/solution.py
+++ b/solution.py
@@ -151,7 +151,7 @@
         class_onehot(neighbours, COARSE),
         precision=highest,
     )
-    coarse = lax.psum(jnp.diag(diagonal_terms) - coupling, ("gx", "gy", "gz"))
+    coarse = lax.psum(lax.psum(jnp.diag(diagonal_terms) - coupling, ("gy", "gz")), "gx")
     coarse = 0.5 * (coarse + coarse.T)
     factor_lower = jnp.linalg.cholesky(coarse)
 

time: 367 us -> 431 us (1.17)
  blocking collectives: 179 us -> 246 us
    psum x1 -> x2, blocking collectives: 40.9 us -> 82.7 us  [coarse_solve(): projected = lax.psum(restrict(field), ('gx', 'gy', 'gz'))]
    psum x1 -> x2, blocking collectives: 40.4 us -> 67.5 us  [the longest x1 60.6 us: body(): lax.psum(jnp.diag(diagonal_terms) - coupling, ('gy', 'gz'))]
  transfers between devices with their start and end apart: 42 -> 42, of which waited for: 16 -> 15; matrix products, arithmetic and copies ran while one was open for 1% -> 1% of each run, Pallas kernels for 0% -> 0%
where the time goes in v1:
time: 431 us; the launch traced here: 429 us
  blocking collectives  246 us (57%)
  starting transfers between devices  112 us (26%)
  other arithmetic  22.3 us (5%)
  waiting for transfers between devices  21.9 us (5%)
  matrix products  13.4 us (3%)
  between operations  8.3 us (2%)
  local copies, waits for them, and re-layouts  5.09 us (1%)
    psum x2, blocking collectives, joint_terms(): lax.psum((restrict(product), jnp.sum(field * field), jnp.sum(field * prod...  95.8 us
    ppermute x21, starting transfers between devices, padded_2(): lax.ppermute(tail, axis, [(i, (i + 1) % count) for i in range(ends)])  84.7 us
    psum x2, blocking collectives, coarse_solve(): projected = lax.psum(restrict(field), ('gx', 'gy', 'gz'))  82.7 us
    psum x1, blocking collectives, body(): lax.psum(jnp.diag(diagonal_terms) - coupling, ('gy', 'gz'))  60.6 us
    ppermute x21, starting transfers between devices, padded_2(): lax.ppermute(head, axis, [((i + 1) % count, i) for i in range(ends)])  27.1 us
    ppermute x21, waiting for transfers between devices, padded_2(): lax.ppermute(tail, axis, [(i, (i + 1) % count) for i in range(ends)])  13.9 us
  transfers between devices with their start and end apart: 42, of which 15 were waited for; matrix products, arithmetic and copies ran while one was open for 1% of the time, Pallas kernels for 0%

profile of v1, /device:TPU:0, one launch (start us, length us, event | category | flops | bytes accessed | tf_op | source)
XLA Modules:
  0.0 428.9 jit_solution(11072835120044480315)
XLA Ops:
  0.6 0.9 slice_bitcast_fusion.11
  1.6 1.7 select_reduce_fusion
  4.2 4.9 %collective-permute-start = (f32[6,1,16,128]{3,2,1,0:T(8,128)S(1)}, f32[6,1,16,128]{3,2,1,0:T(8,128)S(1)}, u32[]{:S(2)}, u32[]{:S(2)}) collective-permute-start(f32[6,1,16,128]{3,2,1,0:T(8,128)S(1)} %get-tuple-element.37), channel_id=1, source_target_pairs={{0,16},{1,17},{2,18},{3,19},{4,20},{5,21},{6,22},{7,23},{8,24},{9,... | collective-permute-start | bytes 147464 | tf_op jit(solution)/shard_map/ppermute | solution.py:44
  9.1 1.3 collective-permute-start.1
  11.4 3.7 collective-permute-done.1
  15.1 3.5 collective-permute-start.2
  18.6 1.3 collective-permute-start.3
  20.2 4.2 collective-permute-done.3
  25.2 1.3 collective-permute-start.4
  27.0 1.3 collective-permute-start.5
  28.3 42.0 %psum.72 = f32[64]{0:T(128)S(1)} all-reduce(f32[64]{0:T(128)S(1)} %convolution_bitcast_fusion.26), channel_id=1, replica_groups=mesh['gx'=2,'gy'=4,'gz'=4] {'gx','gy','gz'}, use_global_device_ids=true, to_apply=%region_13.14 | all-reduce | flops 64 | bytes 512 | tf_op jit(solution)/shard_map/psum | solution.py:171
  82.4 60.6 %psum.70 = f32[64,64]{1,0:T(8,128)S(1)} all-reduce(f32[64,64]{1,0:T(8,128)S(1)} %convolution_subtract_fusion), channel_id=1, replica_groups=mesh['gx'=2,'gy'=4,'gz'=4] {'gy','gz'}, use_global_device_ids=true, to_apply=%region_7.8 | all-reduce | flops 4096 | bytes 32768 | tf_op jit(solution)/shard_map/psum | solution.py:154
  143.0 6.9 %psum.71 = f32[64,64]{1,0:T(8,128)S(1)} all-reduce(f32[64,64]{1,0:T(8,128)S(1)} %psum.70), channel_id=1, replica_groups=mesh['gx'=2,'gy'=4,'gz'=4] {'gx'}, use_global_device_ids=true, to_apply=%region_8.9 | all-reduce | flops 4096 | bytes 32768 | tf_op jit(solution)/shard_map/psum | solution.py:154
  150.1 5.8 %cholesky.19 = f32[64,64]{1,0:T(8,128)S(1)} custom-call(f32[64,64]{1,0:T(8,128)S(1)} %fusion.262), custom_call_target="Cholesky" | custom-call | tf_op jit(solution)/shard_map/jit(cholesky)/cholesky | solution.py:156
  157.3 4.9 %custom-call.11 = f32[1,64,64]{1,2,0:T(8,128)S(1)} custom-call(f32[1,64,64]{2,1,0:T(8,128)S(1)} %fusion.251), custom_call_target="InvertDiagBlocksLowerTriangular" | custom-call | tf_op jit(solution)/shard_map/jit(_cho_solve)/triangular_solve | solution.py:172
  162.9 1.3 collective-permute-start.6
  164.2 4.5 %collective-permute-start.7 = (f32[1,16,128]{2,1,0:T(8,128)S(1)}, f32[1,16,128]{2,1,0:T(8,128)S(1)}, u32[]{:S(2)}, u32[]{:S(2)}) collective-permute-start(f32[1,16,128]{2,1,0:T(8,128)S(1)} %slice.1082), channel_id=1, source_target_pairs={{0,16},{1,17},{2,18},{3,19},{4,20},{5,21},{6,22},{7,23},{8,24},{9,... | collective-permute-start | bytes 24584 | tf_op jit(solution)/shard_map/ppermute | solution.py:44
  168.7 1.3 collective-permute-done.7
  170.1 1.3 collective-permute-start.8
  171.4 4.5 %collective-permute-start.9 = (f32[10,1,128]{2,1,0:T(1,128)S(1)}, f32[10,1,128]{2,1,0:T(1,128)S(1)}, u32[]{:S(2)}, u32[]{:S(2)}) collective-permute-start(f32[10,1,128]{2,1,0:T(1,128)S(1)} %get-tuple-element.103), channel_id=1, source_target_pairs={{0,4},{4,8},{8,12},{1,5},{5,9},{9,13},{2,6},{6,10},{10,14},{3,7},{... | collective-permute-start | bytes 15368 | tf_op jit(solution)/shard_map/ppermute | solution.py:44
  176.0 1.3 collective-permute-done.9
  177.4 1.3 collective-permute-start.10
  178.7 3.0 collective-permute-start.11
  181.8 0.9 collective-permute-done.11
  183.1 1.3 collective-permute-start.12
  184.4 4.5 %collective-permute-start.13 = (f32[1,16,128]{2,1,0:T(8,128)S(1)}, f32[1,16,128]{2,1,0:T(8,128)S(1)}, u32[]{:S(2)}, u32[]{:S(2)}) collective-permute-start(f32[1,16,128]{2,1,0:T(8,128)S(1)} %get-tuple-element.109), channel_id=1, source_target_pairs={{0,16},{1,17},{2,18},{3,19},{4,20},{5,21},{6,22},{7,23},{8,24},{9,... | collective-permute-start | bytes 24584 | tf_op jit(solution)/shard_map/ppermute | solution.py:44
  189.0 1.3 collective-permute-done.13
  190.3 1.3 collective-permute-start.14
  191.6 4.8 %collective-permute-start.15 = (f32[10,1,128]{2,1,0:T(1,128)S(1)}, f32[10,1,128]{2,1,0:T(1,128)S(1)}, u32[]{:S(2)}, u32[]{:S(2)}) collective-permute-start(f32[10,1,128]{2,1,0:T(1,128)S(1)} %get-tuple-element.99), channel_id=1, source_target_pairs={{0,4},{4,8},{8,12},{1,5},{5,9},{9,13},{2,6},{6,10},{10,14},{3,7},{... | collective-permute-start | bytes 15368 | tf_op jit(solution)/shard_map/ppermute | solution.py:44
  196.4 1.3 collective-permute-done.15
  197.9 1.3 collective-permute-start.16
  199.2 3.2 collective-permute-start.17
  204.6 47.2 %all-reduce.2 = (f32[64]{0:T(128)S(1)}, f32[]{:T(128)}, f32[]{:T(128)}) all-reduce(f32[64]{0:T(128)S(1)} %convolution_bitcast_fusion.24, f32[]{:T(128)} %get-tuple-element.10, f32[]{:T(128)} %get-tuple-element.8), channel_id=1, replica_groups=mesh['gx'=2,'gy'=4,'gz'=4] {'gx','gy','gz'}, use_global_device_ids=true, to_apply=%region_20.22 | all-reduce | flops 66 | bytes 528 | tf_op jit(solution)/shard_map/psum | solution.py:185
  253.1 1.3 collective-permute-start.18
  254.4 4.5 %collective-permute-start.19 = (f32[1,16,128]{2,1,0:T(8,128)S(1)}, f32[1,16,128]{2,1,0:T(8,128)S(1)}, u32[]{:S(2)}, u32[]{:S(2)}) collective-permute-start(f32[1,16,128]{2,1,0:T(8,128)S(1)} %slice.1129), channel_id=1, source_target_pairs={{0,16},{1,17},{2,18},{3,19},{4,20},{5,21},{6,22},{7,23},{8,24},{9,... | collective-permute-start | bytes 24584 | tf_op jit(solution)/shard_map/ppermute | solution.py:44
  259.0 1.3 collective-permute-done.19
  260.3 1.3 collective-permute-start.20
  261.6 4.5 %collective-permute-start.21 = (f32[10,1,128]{2,1,0:T(1,128)S(1)}, f32[10,1,128]{2,1,0:T(1,128)S(1)}, u32[]{:S(2)}, u32[]{:S(2)}) collective-permute-start(f32[10,1,128]{2,1,0:T(1,128)S(1)} %get-tuple-element.95), channel_id=1, source_target_pairs={{0,4},{4,8},{8,12},{1,5},{5,9},{9,13},{2,6},{6,10},{10,14},{3,7},{... | collective-permute-start | bytes 15368 | tf_op jit(solution)/shard_map/ppermute | solution.py:44
  268.3 1.3 collective-permute-start.22
  269.6 3.0 collective-permute-start.23
  272.6 0.9 collective-permute-done.23
  274.0 1.3 collective-permute-start.24
  275.3 4.5 %collective-permute-start.25 = (f32[1,16,128]{2,1,0:T(8,128)S(1)}, f32[1,16,128]{2,1,0:T(8,128)S(1)}, u32[]{:S(2)}, u32[]{:S(2)}) collective-permute-start(f32[1,16,128]{2,1,0:T(8,128)S(1)} %get-tuple-element.107), channel_id=1, source_target_pairs={{0,16},{1,17},{2,18},{3,19},{4,20},{5,21},{6,22},{7,23},{8,24},{9,... | collective-permute-start | bytes 24584 | tf_op jit(solution)/shard_map/ppermute | solution.py:44
  279.8 1.3 collective-permute-done.25
  281.2 1.3 collective-permute-start.26
  282.5 4.5 %collective-permute-start.27 = (f32[10,1,128]{2,1,0:T(1,128)S(1)}, f32[10,1,128]{2,1,0:T(1,128)S(1)}, u32[]{:S(2)}, u32[]{:S(2)}) collective-permute-start(f32[10,1,128]{2,1,0:T(1,128)S(1)} %get-tuple-element.91), channel_id=1, source_target_pairs={{0,4},{4,8},{8,12},{1,5},{5,9},{9,13},{2,6},{6,10},{10,14},{3,7},{... | collective-permute-start | bytes 15368 | tf_op jit(solution)/shard_map/ppermute | solution.py:44
  287.0 1.3 collective-permute-done.27
  288.5 1.3 collective-permute-start.28
  289.8 3.2 collective-permute-start.29
  293.1 0.9 collective-permute-done.29
  295.4 48.6 %all-reduce.1 = (f32[]{:T(128)}, f32[]{:T(128)}, f32[64]{0:T(128)S(1)}) all-reduce(f32[]{:T(128)} %get-tuple-element.7, f32[]{:T(128)} %get-tuple-element.6, f32[64]{0:T(128)S(1)} %convolution_bitcast_fusion.22), channel_id=1, replica_groups=mesh['gx'=2,'gy'=4,'gz'=4] {'gx','gy','gz'}, use_global_device_ids=true, to_apply=%region_23.25 | all-reduce | flops 66 | bytes 528 | tf_op jit(solution)/shard_map/psum | solution.py:185
  345.4 1.3 collective-permute-start.36
  346.7 4.5 %collective-permute-start.37 = (f32[1,16,128]{2,1,0:T(8,128)S(1)}, f32[1,16,128]{2,1,0:T(8,128)S(1)}, u32[]{:S(2)}, u32[]{:S(2)}) collective-permute-start(f32[1,16,128]{2,1,0:T(8,128)S(1)} %slice.1200), channel_id=1, source_target_pairs={{0,16},{1,17},{2,18},{3,19},{4,20},{5,21},{6,22},{7,23},{8,24},{9,... | collective-permute-start | bytes 24584 | tf_op jit(solution)/shard_map/ppermute | solution.py:44
  355.8 1.3 collective-permute-start.30
  357.1 4.5 %collective-permute-start.31 = (f32[1,16,128]{2,1,0:T(8,128)S(1)}, f32[1,16,128]{2,1,0:T(8,128)S(1)}, u32[]{:S(2)}, u32[]{:S(2)}) collective-permute-start(f32[1,16,128]{2,1,0:T(8,128)S(1)} %get-tuple-element.105), channel_id=1, source_target_pairs={{0,16},{1,17},{2,18},{3,19},{4,20},{5,21},{6,22},{7,23},{8,24},{9,... | collective-permute-start | bytes 24584 | tf_op jit(solution)/shard_map/ppermute | solution.py:44
  361.7 1.3 collective-permute-start.38
  363.0 4.5 %collective-permute-start.39 = (f32[10,1,128]{2,1,0:T(1,128)S(1)}, f32[10,1,128]{2,1,0:T(1,128)S(1)}, u32[]{:S(2)}, u32[]{:S(2)}) collective-permute-start(f32[10,1,128]{2,1,0:T(1,128)S(1)} %get-tuple-element.83), channel_id=1, source_target_pairs={{0,4},{4,8},{8,12},{1,5},{5,9},{9,13},{2,6},{6,10},{10,14},{3,7},{... | collective-permute-start | bytes 15368 | tf_op jit(solution)/shard_map/ppermute | solution.py:44
  367.6 1.3 collective-permute-start.32
  368.9 4.5 %collective-permute-start.33 = (f32[10,1,128]{2,1,0:T(1,128)S(1)}, f32[10,1,128]{2,1,0:T(1,128)S(1)}, u32[]{:S(2)}, u32[]{:S(2)}) collective-permute-start(f32[10,1,128]{2,1,0:T(1,128)S(1)} %get-tuple-element.87), channel_id=1, source_target_pairs={{0,4},{4,8},{8,12},{1,5},{5,9},{9,13},{2,6},{6,10},{10,14},{3,7},{... | collective-permute-start | bytes 15368 | tf_op jit(solution)/shard_map/ppermute | solution.py:44
  373.6 1.3 collective-permute-start.40
  374.9 3.0 collective-permute-start.41
  378.1 1.3 collective-permute-start.34
  379.4 4.7 %collective-permute-start.35 = (f32[10,18,1]{2,1,0:T(8,128)S(1)}, f32[10,18,1]{2,1,0:T(8,128)S(1)}, u32[]{:S(2)}, u32[]{:S(2)}) collective-permute-start(f32[10,18,1]{2,1,0:T(8,128)S(1)} %get-tuple-element.59), channel_id=1, source_target_pairs={{0,1},{1,2},{2,3},{4,5},{5,6},{6,7},{8,9},{9,10},{10,11},{12,13},{... | collective-permute-start | bytes 2168 | tf_op jit(solution)/shard_map/ppermute | solution.py:44
  385.8 40.7 %psum.79 = f32[64]{0:T(128)S(1)} all-reduce(f32[64]{0:T(128)S(1)} %convolution_bitcast_fusion.21), channel_id=1, replica_groups=mesh['gx'=2,'gy'=4,'gz'=4] {'gx','gy','gz'}, use_global_device_ids=true, to_apply=%region_32.34 | all-reduce | flops 64 | bytes 512 | tf_op jit(solution)/shard_map/psum | solution.py:171
  (218 shorter events, 29.5 us)
Async XLA Ops:
  0.6 10.1 %copy-start = (f32[8,16,128]{2,1,0:T(8,128)S(1)}, f32[8,16,128]{2,1,0:T(8,128)}, u32[]{:S(2)}) copy-start(f32[8,16,128]{2,1,0:T(8,128)} %param.7) | copy-start | bytes 196612
  0.6 10.3 %copy-start.1 = (s32[2,4,8]{2,1,0:T(4,128)S(1)}, s32[2,4,8]{2,1,0:T(4,128)}, u32[]{:S(2)}) copy-start(s32[2,4,8]{2,1,0:T(4,128)} %param.11) | copy-start | bytes 772
  4.2 7.1 %collective-permute-start = (f32[6,1,16,128]{3,2,1,0:T(8,128)S(1)}, f32[6,1,16,128]{3,2,1,0:T(8,128)S(1)}, u32[]{:S(2)}, u32[]{:S(2)}) collective-permute-start(f32[6,1,16,128]{3,2,1,0:T(8,128)S(1)} %get-tuple-element.37), channel_id=1, source_target_pairs={{0,16},{1,17},{2,18},{3,19},{4,20},{5,21},{6,22},{7,23},{8,24},{9,... | collective-permute-start | bytes 147464 | tf_op jit(solution)/shard_map/ppermute | solution.py:44
  9.1 6.0 %collective-permute-start.1 = (f32[6,1,16,128]{3,2,1,0:T(8,128)S(1)}, f32[6,1,16,128]{3,2,1,0:T(8,128)S(1)}, u32[]{:S(2)}, u32[]{:S(2)}) collective-permute-start(f32[6,1,16,128]{3,2,1,0:T(8,128)S(1)} %get-tuple-element.38), channel_id=1, source_target_pairs={{16,0},{17,1},{18,2},{19,3},{20,4},{21,5},{22,6},{23,7},{24,8},{25... | collective-permute-start | bytes 147464 | tf_op jit(solution)/shard_map/ppermute | solution.py:46
  15.1 5.0 %collective-permute-start.2 = (f32[6,10,1,128]{3,2,1,0:T(1,128)S(1)}, f32[6,10,1,128]{3,2,1,0:T(1,128)S(1)}, u32[]{:S(2)}, u32[]{:S(2)}) collective-permute-start(f32[6,10,1,128]{3,2,1,0:T(1,128)S(1)} %get-tuple-element.35), channel_id=1, source_target_pairs={{0,4},{4,8},{8,12},{1,5},{5,9},{9,13},{2,6},{6,10},{10,14},{3,7},{... | collective-permute-start | bytes 92168 | tf_op jit(solution)/shard_map/ppermute | solution.py:44
  18.6 5.8 %collective-permute-start.3 = (f32[6,10,1,128]{3,2,1,0:T(1,128)S(1)}, f32[6,10,1,128]{3,2,1,0:T(1,128)S(1)}, u32[]{:S(2)}, u32[]{:S(2)}) collective-permute-start(f32[6,10,1,128]{3,2,1,0:T(1,128)S(1)} %get-tuple-element.36), channel_id=1, source_target_pairs={{4,0},{8,4},{12,8},{5,1},{9,5},{13,9},{6,2},{10,6},{14,10},{7,3},{... | collective-permute-start | bytes 92168 | tf_op jit(solution)/shard_map/ppermute | solution.py:46
  25.2 45.1 %collective-permute-start.4 = (f32[6,10,18,1]{2,3,1,0:T(1,128)S(1)}, f32[6,10,18,1]{2,3,1,0:T(1,128)S(1)}, u32[]{:S(2)}, u32[]{:S(2)}) collective-permute-start(f32[6,10,18,1]{2,3,1,0:T(1,128)S(1)} %copy.83), channel_id=1, source_target_pairs={{0,1},{1,2},{2,3},{4,5},{5,6},{6,7},{8,9},{9,10},{10,11},{12,13},{... | collective-permute-start | bytes 12968 | tf_op jit(solution)/shard_map/ppermute | solution.py:44
  27.0 43.8 %collective-permute-start.5 = (f32[6,10,18,1]{2,3,1,0:T(1,128)S(1)}, f32[6,10,18,1]{2,3,1,0:T(1,128)S(1)}, u32[]{:S(2)}, u32[]{:S(2)}) collective-permute-start(f32[6,10,18,1]{2,3,1,0:T(1,128)S(1)} %copy.84), channel_id=1, source_target_pairs={{1,0},{2,1},{3,2},{5,4},{6,5},{7,6},{9,8},{10,9},{11,10},{13,12},{... | collective-permute-start | bytes 12968 | tf_op jit(solution)/shard_map/ppermute | solution.py:46
  162.9 5.9 %collective-permute-start.6 = (f32[1,16,128]{2,1,0:T(8,128)S(1)}, f32[1,16,128]{2,1,0:T(8,128)S(1)}, u32[]{:S(2)}, u32[]{:S(2)}) collective-permute-start(f32[1,16,128]{2,1,0:T(8,128)S(1)} %slice.1082), channel_id=1, source_target_pairs={{16,0},{17,1},{18,2},{19,3},{20,4},{21,5},{22,6},{23,7},{24,8},{25... | collective-permute-start | bytes 24584 | tf_op jit(solution)/shard_map/ppermute | solution.py:46
  164.2 5.9 %collective-permute-start.7 = (f32[1,16,128]{2,1,0:T(8,128)S(1)}, f32[1,16,128]{2,1,0:T(8,128)S(1)}, u32[]{:S(2)}, u32[]{:S(2)}) collective-permute-start(f32[1,16,128]{2,1,0:T(8,128)S(1)} %slice.1082), channel_id=1, source_target_pairs={{0,16},{1,17},{2,18},{3,19},{4,20},{5,21},{6,22},{7,23},{8,24},{9,... | collective-permute-start | bytes 24584 | tf_op jit(solution)/shard_map/ppermute | solution.py:44
  170.1 5.9 %collective-permute-start.8 = (f32[10,1,128]{2,1,0:T(1,128)S(1)}, f32[10,1,128]{2,1,0:T(1,128)S(1)}, u32[]{:S(2)}, u32[]{:S(2)}) collective-permute-start(f32[10,1,128]{2,1,0:T(1,128)S(1)} %get-tuple-element.104), channel_id=1, source_target_pairs={{4,0},{8,4},{12,8},{5,1},{9,5},{13,9},{6,2},{10,6},{14,10},{7,3},{... | collective-permute-start | bytes 15368 | tf_op jit(solution)/shard_map/ppermute | solution.py:46
  171.4 5.9 %collective-permute-start.9 = (f32[10,1,128]{2,1,0:T(1,128)S(1)}, f32[10,1,128]{2,1,0:T(1,128)S(1)}, u32[]{:S(2)}, u32[]{:S(2)}) collective-permute-start(f32[10,1,128]{2,1,0:T(1,128)S(1)} %get-tuple-element.103), channel_id=1, source_target_pairs={{0,4},{4,8},{8,12},{1,5},{5,9},{9,13},{2,6},{6,10},{10,14},{3,7},{... | collective-permute-start | bytes 15368 | tf_op jit(solution)/shard_map/ppermute | solution.py:44
  177.4 4.4 %collective-permute-start.10 = (f32[10,18,1]{2,1,0:T(8,128)S(1)}, f32[10,18,1]{2,1,0:T(8,128)S(1)}, u32[]{:S(2)}, u32[]{:S(2)}) collective-permute-start(f32[10,18,1]{2,1,0:T(8,128)S(1)} %get-tuple-element.68), channel_id=1, source_target_pairs={{1,0},{2,1},{3,2},{5,4},{6,5},{7,6},{9,8},{10,9},{11,10},{13,12},{... | collective-permute-start | bytes 2168 | tf_op jit(solution)/shard_map/ppermute | solution.py:46
  178.7 4.0 collective-permute-start.11
  183.1 5.9 %collective-permute-start.12 = (f32[1,16,128]{2,1,0:T(8,128)S(1)}, f32[1,16,128]{2,1,0:T(8,128)S(1)}, u32[]{:S(2)}, u32[]{:S(2)}) collective-permute-start(f32[1,16,128]{2,1,0:T(8,128)S(1)} %get-tuple-element.110), channel_id=1, source_target_pairs={{16,0},{17,1},{18,2},{19,3},{20,4},{21,5},{22,6},{23,7},{24,8},{25... | collective-permute-start | bytes 24584 | tf_op jit(solution)/shard_map/ppermute | solution.py:46
  184.4 5.9 %collective-permute-start.13 = (f32[1,16,128]{2,1,0:T(8,128)S(1)}, f32[1,16,128]{2,1,0:T(8,128)S(1)}, u32[]{:S(2)}, u32[]{:S(2)}) collective-permute-start(f32[1,16,128]{2,1,0:T(8,128)S(1)} %get-tuple-element.109), channel_id=1, source_target_pairs={{0,16},{1,17},{2,18},{3,19},{4,20},{5,21},{6,22},{7,23},{8,24},{9,... | collective-permute-start | bytes 24584 | tf_op jit(solution)/shard_map/ppermute | solution.py:44
  190.3 6.1 %collective-permute-start.14 = (f32[10,1,128]{2,1,0:T(1,128)S(1)}, f32[10,1,128]{2,1,0:T(1,128)S(1)}, u32[]{:S(2)}, u32[]{:S(2)}) collective-permute-start(f32[10,1,128]{2,1,0:T(1,128)S(1)} %get-tuple-element.100), channel_id=1, source_target_pairs={{4,0},{8,4},{12,8},{5,1},{9,5},{13,9},{6,2},{10,6},{14,10},{7,3},{... | collective-permute-start | bytes 15368 | tf_op jit(solution)/shard_map/ppermute | solution.py:46
  191.6 6.1 %collective-permute-start.15 = (f32[10,1,128]{2,1,0:T(1,128)S(1)}, f32[10,1,128]{2,1,0:T(1,128)S(1)}, u32[]{:S(2)}, u32[]{:S(2)}) collective-permute-start(f32[10,1,128]{2,1,0:T(1,128)S(1)} %get-tuple-element.99), channel_id=1, source_target_pairs={{0,4},{4,8},{8,12},{1,5},{5,9},{9,13},{2,6},{6,10},{10,14},{3,7},{... | collective-permute-start | bytes 15368 | tf_op jit(solution)/shard_map/ppermute | solution.py:44
  197.9 4.6 %collective-permute-start.16 = (f32[10,18,1]{2,1,0:T(8,128)S(1)}, f32[10,18,1]{2,1,0:T(8,128)S(1)}, u32[]{:S(2)}, u32[]{:S(2)}) collective-permute-start(f32[10,18,1]{2,1,0:T(8,128)S(1)} %get-tuple-element.66), channel_id=1, source_target_pairs={{1,0},{2,1},{3,2},{5,4},{6,5},{7,6},{9,8},{10,9},{11,10},{13,12},{... | collective-permute-start | bytes 2168 | tf_op jit(solution)/shard_map/ppermute | solution.py:46
  199.2 4.0 collective-permute-start.17
  253.1 5.8 %collective-permute-start.18 = (f32[1,16,128]{2,1,0:T(8,128)S(1)}, f32[1,16,128]{2,1,0:T(8,128)S(1)}, u32[]{:S(2)}, u32[]{:S(2)}) collective-permute-start(f32[1,16,128]{2,1,0:T(8,128)S(1)} %slice.1129), channel_id=1, source_target_pairs={{16,0},{17,1},{18,2},{19,3},{20,4},{21,5},{22,6},{23,7},{24,8},{25... | collective-permute-start | bytes 24584 | tf_op jit(solution)/shard_map/ppermute | solution.py:46
  254.4 5.9 %collective-permute-start.19 = (f32[1,16,128]{2,1,0:T(8,128)S(1)}, f32[1,16,128]{2,1,0:T(8,128)S(1)}, u32[]{:S(2)}, u32[]{:S(2)}) collective-permute-start(f32[1,16,128]{2,1,0:T(8,128)S(1)} %slice.1129), channel_id=1, source_target_pairs={{0,16},{1,17},{2,18},{3,19},{4,20},{5,21},{6,22},{7,23},{8,24},{9,... | collective-permute-start | bytes 24584 | tf_op jit(solution)/shard_map/ppermute | solution.py:44
  260.3 7.8 %collective-permute-start.20 = (f32[10,1,128]{2,1,0:T(1,128)S(1)}, f32[10,1,128]{2,1,0:T(1,128)S(1)}, u32[]{:S(2)}, u32[]{:S(2)}) collective-permute-start(f32[10,1,128]{2,1,0:T(1,128)S(1)} %get-tuple-element.96), channel_id=1, source_target_pairs={{4,0},{8,4},{12,8},{5,1},{9,5},{13,9},{6,2},{10,6},{14,10},{7,3},{... | collective-permute-start | bytes 15368 | tf_op jit(solution)/shard_map/ppermute | solution.py:46
  261.6 6.5 %collective-permute-start.21 = (f32[10,1,128]{2,1,0:T(1,128)S(1)}, f32[10,1,128]{2,1,0:T(1,128)S(1)}, u32[]{:S(2)}, u32[]{:S(2)}) collective-permute-start(f32[10,1,128]{2,1,0:T(1,128)S(1)} %get-tuple-element.95), channel_id=1, source_target_pairs={{0,4},{4,8},{8,12},{1,5},{5,9},{9,13},{2,6},{6,10},{10,14},{3,7},{... | collective-permute-start | bytes 15368 | tf_op jit(solution)/shard_map/ppermute | solution.py:44
  268.3 4.4 %collective-permute-start.22 = (f32[10,18,1]{2,1,0:T(8,128)S(1)}, f32[10,18,1]{2,1,0:T(8,128)S(1)}, u32[]{:S(2)}, u32[]{:S(2)}) collective-permute-start(f32[10,18,1]{2,1,0:T(8,128)S(1)} %get-tuple-element.64), channel_id=1, source_target_pairs={{1,0},{2,1},{3,2},{5,4},{6,5},{7,6},{9,8},{10,9},{11,10},{13,12},{... | collective-permute-start | bytes 2168 | tf_op jit(solution)/shard_map/ppermute | solution.py:46
  269.6 4.0 collective-permute-start.23
  274.0 5.9 %collective-permute-start.24 = (f32[1,16,128]{2,1,0:T(8,128)S(1)}, f32[1,16,128]{2,1,0:T(8,128)S(1)}, u32[]{:S(2)}, u32[]{:S(2)}) collective-permute-start(f32[1,16,128]{2,1,0:T(8,128)S(1)} %get-tuple-element.108), channel_id=1, source_target_pairs={{16,0},{17,1},{18,2},{19,3},{20,4},{21,5},{22,6},{23,7},{24,8},{25... | collective-permute-start | bytes 24584 | tf_op jit(solution)/shard_map/ppermute | solution.py:46
  275.3 5.9 %collective-permute-start.25 = (f32[1,16,128]{2,1,0:T(8,128)S(1)}, f32[1,16,128]{2,1,0:T(8,128)S(1)}, u32[]{:S(2)}, u32[]{:S(2)}) collective-permute-start(f32[1,16,128]{2,1,0:T(8,128)S(1)} %get-tuple-element.107), channel_id=1, source_target_pairs={{0,16},{1,17},{2,18},{3,19},{4,20},{5,21},{6,22},{7,23},{8,24},{9,... | collective-permute-start | bytes 24584 | tf_op jit(solution)/shard_map/ppermute | solution.py:44
  281.2 5.9 %collective-permute-start.26 = (f32[10,1,128]{2,1,0:T(1,128)S(1)}, f32[10,1,128]{2,1,0:T(1,128)S(1)}, u32[]{:S(2)}, u32[]{:S(2)}) collective-permute-start(f32[10,1,128]{2,1,0:T(1,128)S(1)} %get-tuple-element.92), channel_id=1, source_target_pairs={{4,0},{8,4},{12,8},{5,1},{9,5},{13,9},{6,2},{10,6},{14,10},{7,3},{... | collective-permute-start | bytes 15368 | tf_op jit(solution)/shard_map/ppermute | solution.py:46
  282.5 5.9 %collective-permute-start.27 = (f32[10,1,128]{2,1,0:T(1,128)S(1)}, f32[10,1,128]{2,1,0:T(1,128)S(1)}, u32[]{:S(2)}, u32[]{:S(2)}) collective-permute-start(f32[10,1,128]{2,1,0:T(1,128)S(1)} %get-tuple-element.91), channel_id=1, source_target_pairs={{0,4},{4,8},{8,12},{1,5},{5,9},{9,13},{2,6},{6,10},{10,14},{3,7},{... | collective-permute-start | bytes 15368 | tf_op jit(solution)/shard_map/ppermute | solution.py:44
  288.5 4.6 %collective-permute-start.28 = (f32[10,18,1]{2,1,0:T(8,128)S(1)}, f32[10,18,1]{2,1,0:T(8,128)S(1)}, u32[]{:S(2)}, u32[]{:S(2)}) collective-permute-start(f32[10,18,1]{2,1,0:T(8,128)S(1)} %get-tuple-element.62), channel_id=1, source_target_pairs={{1,0},{2,1},{3,2},{5,4},{6,5},{7,6},{9,8},{10,9},{11,10},{13,12},{... | collective-permute-start | bytes 2168 | tf_op jit(solution)/shard_map/ppermute | solution.py:46
  289.8 4.2 collective-permute-start.29
  345.4 16.3 %collective-permute-start.36 = (f32[1,16,128]{2,1,0:T(8,128)S(1)}, f32[1,16,128]{2,1,0:T(8,128)S(1)}, u32[]{:S(2)}, u32[]{:S(2)}) collective-permute-start(f32[1,16,128]{2,1,0:T(8,128)S(1)} %slice.1200), channel_id=1, source_target_pairs={{16,0},{17,1},{18,2},{19,3},{20,4},{21,5},{22,6},{23,7},{24,8},{25... | collective-permute-start | bytes 24584 | tf_op jit(solution)/shard_map/ppermute | solution.py:46
  346.7 15.0 %collective-permute-start.37 = (f32[1,16,128]{2,1,0:T(8,128)S(1)}, f32[1,16,128]{2,1,0:T(8,128)S(1)}, u32[]{:S(2)}, u32[]{:S(2)}) collective-permute-start(f32[1,16,128]{2,1,0:T(8,128)S(1)} %slice.1200), channel_id=1, source_target_pairs={{0,16},{1,17},{2,18},{3,19},{4,20},{5,21},{6,22},{7,23},{8,24},{9,... | collective-permute-start | bytes 24584 | tf_op jit(solution)/shard_map/ppermute | solution.py:44
  355.8 11.8 %collective-permute-start.30 = (f32[1,16,128]{2,1,0:T(8,128)S(1)}, f32[1,16,128]{2,1,0:T(8,128)S(1)}, u32[]{:S(2)}, u32[]{:S(2)}) collective-permute-start(f32[1,16,128]{2,1,0:T(8,128)S(1)} %get-tuple-element.106), channel_id=1, source_target_pairs={{16,0},{17,1},{18,2},{19,3},{20,4},{21,5},{22,6},{23,7},{24,8},{25... | collective-permute-start | bytes 24584 | tf_op jit(solution)/shard_map/ppermute | solution.py:46
  357.1 10.5 %collective-permute-start.31 = (f32[1,16,128]{2,1,0:T(8,128)S(1)}, f32[1,16,128]{2,1,0:T(8,128)S(1)}, u32[]{:S(2)}, u32[]{:S(2)}) collective-permute-start(f32[1,16,128]{2,1,0:T(8,128)S(1)} %get-tuple-element.105), channel_id=1, source_target_pairs={{0,16},{1,17},{2,18},{3,19},{4,20},{5,21},{6,22},{7,23},{8,24},{9,... | collective-permute-start | bytes 24584 | tf_op jit(solution)/shard_map/ppermute | solution.py:44
  361.7 11.8 %collective-permute-start.38 = (f32[10,1,128]{2,1,0:T(1,128)S(1)}, f32[10,1,128]{2,1,0:T(1,128)S(1)}, u32[]{:S(2)}, u32[]{:S(2)}) collective-permute-start(f32[10,1,128]{2,1,0:T(1,128)S(1)} %get-tuple-element.84), channel_id=1, source_target_pairs={{4,0},{8,4},{12,8},{5,1},{9,5},{13,9},{6,2},{10,6},{14,10},{7,3},{... | collective-permute-start | bytes 15368 | tf_op jit(solution)/shard_map/ppermute | solution.py:46
  363.0 10.5 %collective-permute-start.39 = (f32[10,1,128]{2,1,0:T(1,128)S(1)}, f32[10,1,128]{2,1,0:T(1,128)S(1)}, u32[]{:S(2)}, u32[]{:S(2)}) collective-permute-start(f32[10,1,128]{2,1,0:T(1,128)S(1)} %get-tuple-element.83), channel_id=1, source_target_pairs={{0,4},{4,8},{8,12},{1,5},{5,9},{9,13},{2,6},{6,10},{10,14},{3,7},{... | collective-permute-start | bytes 15368 | tf_op jit(solution)/shard_map/ppermute | solution.py:44
  367.6 10.3 %collective-permute-start.32 = (f32[10,1,128]{2,1,0:T(1,128)S(1)}, f32[10,1,128]{2,1,0:T(1,128)S(1)}, u32[]{:S(2)}, u32[]{:S(2)}) collective-permute-start(f32[10,1,128]{2,1,0:T(1,128)S(1)} %get-tuple-element.88), channel_id=1, source_target_pairs={{4,0},{8,4},{12,8},{5,1},{9,5},{13,9},{6,2},{10,6},{14,10},{7,3},{... | collective-permute-start | bytes 15368 | tf_op jit(solution)/shard_map/ppermute | solution.py:46
  368.9 9.1 %collective-permute-start.33 = (f32[10,1,128]{2,1,0:T(1,128)S(1)}, f32[10,1,128]{2,1,0:T(1,128)S(1)}, u32[]{:S(2)}, u32[]{:S(2)}) collective-permute-start(f32[10,1,128]{2,1,0:T(1,128)S(1)} %get-tuple-element.87), channel_id=1, source_target_pairs={{0,4},{4,8},{8,12},{1,5},{5,9},{9,13},{2,6},{6,10},{10,14},{3,7},{... | collective-permute-start | bytes 15368 | tf_op jit(solution)/shard_map/ppermute | solution.py:44
  373.6 54.2 %collective-permute-start.40 = (f32[10,18,1]{2,1,0:T(8,128)S(1)}, f32[10,18,1]{2,1,0:T(8,128)S(1)}, u32[]{:S(2)}, u32[]{:S(2)}) collective-permute-start(f32[10,18,1]{2,1,0:T(8,128)S(1)} %get-tuple-element.58), channel_id=1, source_target_pairs={{1,0},{2,1},{3,2},{5,4},{6,5},{7,6},{9,8},{10,9},{11,10},{13,12},{... | collective-permute-start | bytes 2168 | tf_op jit(solution)/shard_map/ppermute | solution.py:46
  374.9 52.9 %collective-permute-start.41 = (f32[10,18,1]{2,1,0:T(8,128)S(1)}, f32[10,18,1]{2,1,0:T(8,128)S(1)}, u32[]{:S(2)}, u32[]{:S(2)}) collective-permute-start(f32[10,18,1]{2,1,0:T(8,128)S(1)} %get-tuple-element.57), channel_id=1, source_target_pairs={{0,1},{1,2},{2,3},{4,5},{5,6},{6,7},{8,9},{9,10},{10,11},{12,13},{... | collective-permute-start | bytes 2168 | tf_op jit(solution)/shard_map/ppermute | solution.py:44
  378.1 6.0 %collective-permute-start.34 = (f32[10,18,1]{2,1,0:T(8,128)S(1)}, f32[10,18,1]{2,1,0:T(8,128)S(1)}, u32[]{:S(2)}, u32[]{:S(2)}) collective-permute-start(f32[10,18,1]{2,1,0:T(8,128)S(1)} %get-tuple-element.60), channel_id=1, source_target_pairs={{1,0},{2,1},{3,2},{5,4},{6,5},{7,6},{9,8},{10,9},{11,10},{13,12},{... | collective-permute-start | bytes 2168 | tf_op jit(solution)/shard_map/ppermute | solution.py:46
  379.4 5.6 %collective-permute-start.35 = (f32[10,18,1]{2,1,0:T(8,128)S(1)}, f32[10,18,1]{2,1,0:T(8,128)S(1)}, u32[]{:S(2)}, u32[]{:S(2)}) collective-permute-start(f32[10,18,1]{2,1,0:T(8,128)S(1)} %get-tuple-element.59), channel_id=1, source_target_pairs={{0,1},{1,2},{2,3},{4,5},{5,6},{6,7},{8,9},{9,10},{10,11},{12,13},{... | collective-permute-start | bytes 2168 | tf_op jit(solution)/shard_map/ppermute | solution.py:44
